TPU v7x, 16 devices: a 4x2x1 block of a 4x4x8 slice. The times are simulated.
16 devices in a mesh: dp: 4 (over y, z, core), tp: 4 (over x).
Axes of the slice: x: 4, y: 2, z: 1, core: 2. Of those that a mesh axis runs over, the one named last changes fastest.
The devices are a block of a 4x4x8 slice.
Arguments:
- x: bfloat16 [4096, 4096], P(('dp', 'tp')), parts along dimension 0
- dy: bfloat16 [4096, 4096], P(('dp', 'tp')), parts along dimension 0
- gate: bfloat16 [4096, 12800], P('dp', 'tp'), parts along dimension 0
- up: bfloat16 [4096, 12800], P('dp', 'tp'), parts along dimension 0
- w_gate: bfloat16 [4096, 12800], P(None, 'tp')
- w_up: bfloat16 [4096, 12800], P(None, 'tp')
- w_down: bfloat16 [12800, 4096], P('tp')
Outputs:
- output 1: bfloat16 [4096, 4096], P(('dp', 'tp')), parts along dimension 0
- output 2: bfloat16 [16384, 12800], P('dp', 'tp'), parts along dimension 0
- output 3: bfloat16 [16384, 12800], P('dp', 'tp'), parts along dimension 0
- output 4: bfloat16 [51200, 4096], P(('dp', 'tp')), parts along dimension 0
There are 4 independent parts. A program takes and returns all parts, laid end to end along the dimension named above; an argument that names none is the same for every part.
All inputs are finite; a program needn't handle non-finite values.
Results may differ from a plain program's by a relative error of at most 0.012.
Values are sent between devices in bfloat16 or wider.
A program may use at most 768 MiB of HBM per device.

v0:
```python
import jax
import jax.numpy as jnp


def act(gate, up):
    return jax.nn.silu(gate) * up


def solution(mesh):
    def step(x, dy, gate, up, w_gate, w_up, w_down):
        hidden, back = jax.vjp(act, gate.astype(jnp.float32), up.astype(jnp.float32))
        d_hidden = jnp.dot(dy, w_down.T, preferred_element_type=jnp.float32)
        d_gate, d_up = (g.astype(jnp.bfloat16) for g in back(d_hidden))
        dx = jnp.dot(d_gate, w_gate.T) + jnp.dot(d_up, w_up.T)
        groups = mesh.shape["dp"]

        def by_group(a, b):
            a, b = (t.reshape(groups, -1, t.shape[-1]) for t in (a, b))
            product = jnp.einsum("gta,gtb->gab", a, b, preferred_element_type=jnp.float32)
            return product.astype(jnp.bfloat16).reshape(-1, b.shape[-1])

        return dx, by_group(x, d_gate), by_group(x, d_up), by_group(hidden.astype(jnp.bfloat16), dy)

    return step
```

profile of v0, /device:TPU:112, one launch (start us, length us, event | category | flops | bytes accessed | tf_op | source)
XLA Modules:
  0.0 474.8 jit_solution(5093392088093879196)
XLA Ops:
  7.2 0.1 all-gather.9.cloned.1.call-start
  7.2 0.7 all-gather.9.cloned.1.call-update
  8.0 0.1 all-gather.11.cloned.1.call-start
  8.0 2.4 collective-permute-start
  10.5 0.1 all-gather.11.cloned.1.call-update
  10.5 0.1 reduce-scatter.4.cloned.1.call-start
  10.6 114.8 %all-gather.9.cloned.1.call-done = bf16[1024,4096]{1,0:T(8,128)(2,1)} async-done(((bf16[256,4096]{1,0:T(8,128)(2,1)}), bf16[1024,4096]{1,0:T(8,128)(2,1)}) %all-gather.9.cloned.1.call-update) | async-done | bytes 8388624 | tf_op args[1]
  125.4 32.2 %fusion.26 = f32[1024,3200]{1,0:T(8,128)S(1)} fusion(bf16[1024,4096]{1,0:T(8,128)(2,1)} %all-gather.9.cloned.1.call-done, bf16[3200,4096]{1,0:T(8,128)(2,1)} %param.3), kind=kOutput, calls=%fused_computation.41 | convolution fusion | flops 26843545600 | bytes 47710208 | tf_op jit(solution)/dot_general | solution.py:12
  157.6 0.0 copy-start
  157.7 15.0 %fusion.10 = (bf16[1,1,1024,3200]{3,2,1,0:T(8,128)(2,1)}, bf16[1024,3200]{1,0:T(8,128)(2,1)S(1)}) fusion(bf16[1024,3200]{1,0:T(8,128)(2,1)} %param.4, bf16[1024,3200]{1,0:T(8,128)(2,1)} %param.5, f32[1024,3200]{1,0:T(8,128)S(1)} %fusion.26), kind=kLoop, calls=%fused_computation.24 | loop fusion | flops 52428800 | bytes 39321600 | tf_op jit(solution)/gta,gtb->gab/dot_general | solution.py:19
  172.6 0.0 copy-done
  172.6 0.0 copy-start.1
  172.6 2.8 copy-done.1
  175.4 33.1 %fusion.27 = bf16[1024,4096]{1,0:T(8,128)(2,1)} fusion(bf16[1024,3200]{1,0:T(8,128)(2,1)S(1)} %get-tuple-element.17, bf16[4096,3200]{1,0:T(8,128)(2,1)} %param.6), kind=kOutput, calls=%fused_computation.42 | convolution fusion | flops 26843545600 | bytes 41156608 | tf_op jit(solution)/dot_general | solution.py:14
  208.5 54.1 %convolution_add_fusion = bf16[1024,4096]{1,0:T(8,128)(2,1)} fusion(bf16[1024,4096]{1,0:T(8,128)(2,1)} %fusion.27, bf16[4096,3200]{1,0:T(8,128)(2,1)} %param.7, f32[1024,3200]{1,0:T(8,128)} %copy-done, bf16[1024,3200]{1,0:T(8,128)(2,1)} %param.5), kind=kOutput, calls=%fused_computation.25 | convolution fusion | flops 26870677504 | bytes 62652416 | tf_op jit(solution)/dot_general | solution.py:14
  262.6 0.0 copy-start.2
  262.6 0.0 copy-start.3
  262.6 0.1 reduce-scatter.4.cloned.1.call-update
  262.7 1.5 copy-done.2
  264.2 1.7 collective-permute-start.1
  265.9 0.0 copy-done.3
  265.9 0.6 dynamic-slice.27
  269.1 0.0 collective-permute-done
  269.1 0.4 collective-permute-start.2
  269.5 0.0 all-gather.11.cloned.1.call-done
  269.5 34.9 %fusion.1 = bf16[4096,3200]{0,1:T(8,128)(2,1)} fusion(bf16[1024,3200]{1,0:T(8,128)(2,1)} %copy-done.1, bf16[1024,4096]{1,0:T(8,128)(2,1)} %all-gather.11.cloned.1.call-done), kind=kOutput, calls=%fused_computation.4 | convolution fusion | flops 26856652800 | bytes 41156608 | tf_op jit(solution)/gta,gtb->gab/dot_general | solution.py:19
  304.4 32.5 %copy.2 = bf16[4096,3200]{1,0:T(8,128)(2,1)} copy(bf16[4096,3200]{0,1:T(8,128)(2,1)} %fusion.1) | data formatting | bytes 52428800
  336.9 43.8 %fusion.2 = bf16[4096,3200]{0,1:T(8,128)(2,1)} fusion(bf16[1024,4096]{1,0:T(8,128)(2,1)} %all-gather.11.cloned.1.call-done, f32[1024,3200]{1,0:T(8,128)} %copy-done, bf16[1024,3200]{1,0:T(8,128)(2,1)} %param.5), kind=kOutput, calls=%fused_computation.5 | convolution fusion | flops 26879590400 | bytes 54263808 | tf_op jit(solution)/gta,gtb->gab/dot_general | solution.py:19
  380.7 32.5 %copy.3 = bf16[4096,3200]{1,0:T(8,128)(2,1)} copy(bf16[4096,3200]{0,1:T(8,128)(2,1)} %fusion.2) | data formatting | bytes 52428800
  413.2 24.8 %fusion.11 = f32[3200,4096,1]{1,0,2:T(8,128)} fusion(bf16[1,1,256,4096]{3,2,1,0:T(8,128)(2,1)} %collective-permute-done, bf16[1,1,256,4096]{3,2,1,0:T(8,128)(2,1)S(1)} %bitcast.48, s32[]{:T(128)} %bitcast.8, bf16[1,1,1024,3200]{3,2,1,0:T(8,128)(2,1)} %get-tuple-element.16, s32[]{:T(128)} %bitcast.9), kind=kOutput, calls=%fused_computation.27 | convolution fusion | flops 13430423552 | bytes 63176712 | tf_op jit(solution)/gta,gtb->gab/dot_general | solution.py:19
  438.0 0.0 collective-permute-done.1
  438.0 0.0 collective-permute-done.2
  438.0 30.0 %fusion = bf16[3200,4096]{1,0:T(8,128)(2,1)} fusion(f32[3200,4096,1]{1,0,2:T(8,128)} %fusion.11, bf16[1,1,256,4096]{3,2,1,0:T(8,128)(2,1)} %collective-permute-done.2, bf16[1,1,256,4096]{3,2,1,0:T(8,128)(2,1)} %collective-permute-done.1, s32[]{:T(128)} %bitcast.14, bf16[1,1,1024,3200]{3,2,1,0:T(8,128)(2,1)} %get-tuple-element.16, s32[]{:T(128)} %bitcast.15), kind=kOutput, calls=%fused_computation.1 | convolution fusion | flops 13456637952 | bytes 89391112 | tf_op jit(solution)/gta,gtb->gab/dot_general | solution.py:19
  468.0 0.0 reduce-scatter.4.cloned.1.call-done
Async XLA Ops:
  7.2 118.2 %all-gather.9.cloned.1.call-start = ((), (), s32[]{:S(2)}) async-start(), calls=%async_computation.1 | async-start | bytes 10485760 | tf_op args[1]
  8.0 261.5 %all-gather.11.cloned.1.call-start = ((), (), s32[]{:S(2)}) async-start(), calls=%async_computation.2 | async-start | bytes 10485760 | tf_op jit(solution)/reshape | solution.py:18
  8.0 261.0 %collective-permute-start = (bf16[1,1,256,4096]{3,2,1,0:T(8,128)(2,1)}, bf16[1,1,256,4096]{3,2,1,0:T(8,128)(2,1)}, u32[]{:S(2)}, u32[]{:S(2)}) collective-permute-start(bf16[1,1,256,4096]{3,2,1,0:T(8,128)(2,1)} %bitcast.46), channel_id=9, source_target_pairs={{0,1},{1,2},{2,3},{3,0},{4,5},{5,6},{6,7},{7,4},{8,9},{9,10},{10,1... | collective-permute-start | bytes 6291464 | tf_op jit(solution)/gta,gtb->gab/dot_general | solution.py:19
  10.5 457.5 %reduce-scatter.4.cloned.1.call-start = ((), (), s32[]{:S(2)}) async-start(), calls=%async_computation.3 | async-start | bytes 10485760
  157.6 15.0 %copy-start = (f32[1024,3200]{1,0:T(8,128)}, f32[1024,3200]{1,0:T(8,128)S(1)}, u32[]{:S(2)}) copy-start(f32[1024,3200]{1,0:T(8,128)S(1)} %fusion.26) | copy-start | bytes 39321604
  172.6 2.8 copy-start.1
  262.6 1.6 copy-start.2
  262.6 3.3 copy-start.3
  264.2 173.8 %collective-permute-start.1 = (bf16[1,1,256,4096]{3,2,1,0:T(8,128)(2,1)S(1)}, bf16[1,1,256,4096]{3,2,1,0:T(8,128)(2,1)}, u32[]{:S(2)}, u32[]{:S(2)}) collective-permute-start(bf16[1,1,256,4096]{3,2,1,0:T(8,128)(2,1)S(1)} %bitcast.47), channel_id=10, source_target_pairs={{0,3},{1,0},{2,1},{3,2},{4,7},{5,4},{6,5},{7,6},{8,11},{9,8},{10,9... | collective-permute-start | bytes 6291464 | tf_op jit(solution)/gta,gtb->gab/dot_general | solution.py:19
  269.1 168.9 %collective-permute-start.2 = (bf16[1,1,256,4096]{3,2,1,0:T(8,128)(2,1)}, bf16[1,1,256,4096]{3,2,1,0:T(8,128)(2,1)}, u32[]{:S(2)}, u32[]{:S(2)}) collective-permute-start(bf16[1,1,256,4096]{3,2,1,0:T(8,128)(2,1)} %collective-permute-done), channel_id=11, source_target_pairs={{0,1},{1,2},{2,3},{3,0},{4,5},{5,6},{6,7},{7,4},{8,9},{9,10},{10,1... | collective-permute-start | bytes 6291464 | tf_op jit(solution)/gta,gtb->gab/dot_general | solution.py:19
Sparse Core Ops, SparseCore 0:
  9.6 115.7 all-gather.8
  126.9 79.9 all-gather.10
  262.8 122.0 reduce-scatter.3
where the time goes:
time: 483 us; the launch traced here: 475 us
  matrix products  253 us (52%)
  waiting for transfers between devices  116 us (24%)
  local copies, waits for them, and re-layouts  69.9 us (14%)
  between operations  16.6 us (3%)
  other arithmetic  15 us (3%)
    dot_general x4, matrix products, by_group(): jnp.einsum('gta,gtb->gab', a, b, preferred_element_type=jnp.float32)  134 us
    unnamed x5, waiting for transfers between devices  116 us
    dot_general x2, matrix products, step(): dx = jnp.dot(d_gate, w_gate.T) + jnp.dot(d_up, w_up.T)  87.2 us
    unnamed x10, local copies, waits for them, and re-layouts  69.3 us
    dot_general x1, matrix products, step(): d_hidden = jnp.dot(dy, w_down.T, preferred_element_type=jnp.float32)  32.2 us
    dot_general x1, other arithmetic, by_group(): jnp.einsum('gta,gtb->gab', a, b, preferred_element_type=jnp.float32)  15 us
  transfers between devices with their start and end apart: 6, of which 1 were waited for; matrix products, arithmetic and copies ran while one was open for 70% of the time, Pallas kernels for 0%

commit v1 on v0

v1 whole, which is shorter than its diff:
```python
import functools

import jax
import jax.numpy as jnp
from jax import lax
from jax.experimental import pallas as pl
from jax.experimental.pallas import tpu as pltpu
from jax.sharding import PartitionSpec as P

BF16, F32 = jnp.bfloat16, jnp.float32
VMEM_LIMIT = 67_000_000


def nt(a, b):
    return lax.dot_general(a, b, (((1,), (1,)), ((), ())), preferred_element_type=F32)


def tn(a, b):
    return lax.dot_general(a, b, (((0,), (0,)), ((), ())), preferred_element_type=F32)


def splits(total, step):
    starts = list(range(0, total, step))
    if len(starts) > 1 and total - starts[-1] < step // 2:
        starts.pop()
    return [(s, e - s) for s, e in zip(starts, starts[1:] + [total])]


def gather_kernel(n, a_tiles, tb, tm, tn_cols, dy0, x0, gate, up, w_down, w_gate, w_up,
                  xg, dg, du, own, mid, raw_l, raw_r, far_0, far_1, dwd,
                  dyg, hid, dgc, duc, gb, ub, xst, wa, wb, st_f, st_b,
                  s_dy, r_dy, s_x, r_x, m_in, m_gu, m_wa, m_wb, m_st, m_d, m_o):
    rows, d = dy0.shape
    ff = gate.shape[1]
    half = rows // 2
    me = lax.axis_index("tp")
    right, left = lax.rem(me + 1, n), lax.rem(me + n - 1, n)
    n_a, n_b = len(a_tiles), d // tb
    chunks = 4

    def place(c, p):
        return pl.ds(pl.multiple_of(c * rows + p * half, half), half)

    def send(src, dst, s_sem, r_sem, c, p, to):
        return pltpu.make_async_remote_copy(src_ref=src, dst_ref=dst.at[place(c, p)], send_sem=s_sem.at[c, p],
                                            recv_sem=r_sem.at[c, p], device_id={"tp": to},
                                            device_id_type=pl.DeviceIdType.MESH)

    def block_sends(src, dst, s_sem, r_sem):
        h0, h1 = src.at[pl.ds(0, half)], src.at[pl.ds(half, half)]
        return [send(h0, dst, s_sem, r_sem, 1, 0, right), send(h1, dst, s_sem, r_sem, 1, 1, left),
                send(h1, dst, s_sem, r_sem, 2, 0, right), send(h0, dst, s_sem, r_sem, 2, 1, left)]

    def forwards(buf, s_sem, r_sem):
        return [send(buf.at[place(1, 0)], buf, s_sem, r_sem, 3, 0, right),
                send(buf.at[place(1, 1)], buf, s_sem, r_sem, 3, 1, left)]

    def arrived(buf, r_sem, c):
        for p in range(2):
            pltpu.make_async_copy(buf.at[place(c, p)], buf.at[place(c, p)], r_sem.at[c, p]).wait()

    def load_a(t, slot):
        start, size = a_tiles[t]
        return pltpu.make_async_copy(w_down.at[pl.ds(start, size)], wa.at[slot, pl.ds(0, size)], m_wa.at[slot])

    def load_b(j, slot):
        at = pl.ds(pl.multiple_of(j * tb, tb), tb)
        return [pltpu.make_async_copy(w.at[at], wb.at[slot, k], m_wb.at[slot, k]) for k, w in enumerate((w_gate, w_up))]

    def load_gu(c):
        later, last = (c + 2) // 3, c // 3
        flip = (c // 2) * (1 - last)
        copies = []
        for p, (shift, h) in enumerate(((later * (n - 1) - last * (n - 3), flip), (later + last, 1 - flip))):
            at = pl.ds(pl.multiple_of(lax.rem(me + shift, n) * rows + h * half, half), half)
            for k, (src, dst) in enumerate(((gate, gb), (up, ub))):
                copies.append(pltpu.make_async_copy(src.at[at], dst.at[pl.ds(p * half, half)], m_gu.at[p, k]))
        return copies

    def save_d(c):
        at = pl.ds(pl.multiple_of(c * rows, rows), rows)
        return [pltpu.make_async_copy(dgc, dg.at[at], m_d.at[0]), pltpu.make_async_copy(duc, du.at[at], m_d.at[1])]

    def save_f(dst, j, slot):
        at = pl.ds(pl.multiple_of(j * tb, tb), tb)
        return pltpu.make_async_copy(st_f.at[slot], dst.at[:, at], m_st.at[slot, 0])

    def save_b(dst0, dst1, j, slot):
        at = pl.ds(pl.multiple_of(j * tb, tb), tb)
        return [pltpu.make_async_copy(st_b.at[slot, pl.ds(p * half, half)], dst.at[:, at], m_st.at[slot, p])
                for p, dst in enumerate((dst0, dst1))]

    first_dy = pltpu.make_async_copy(dy0, dyg.at[pl.ds(0, rows)], m_in.at[0])
    first_x = pltpu.make_async_copy(x0, xst, m_in.at[1])
    keep_x = pltpu.make_async_copy(xst, xg.at[pl.ds(0, rows)], m_in.at[2])
    first_dy.start()
    load_a(0, 0).start()
    for c in load_gu(0):
        c.start()
    first_x.start()
    load_a(1, 1).start()
    for c in load_b(0, 0) + load_b(1, 1):
        c.start()

    barrier = pltpu.get_barrier_semaphore()
    for other in (left, right):
        pl.semaphore_signal(barrier, inc=1, device_id={"tp": other}, device_id_type=pl.DeviceIdType.MESH)
    pl.semaphore_wait(barrier, 2)
    for c in block_sends(dy0, dyg, s_dy, r_dy):
        c.start()
    first_x.wait()
    keep_x.start()
    first_dy.wait()

    def chunk(c, carry):
        @pl.when(c > 0)
        def _():
            arrived(dyg, r_dy, c)

        @pl.when(c == 1)
        def _():
            for k in forwards(dyg, s_dy, r_dy):
                k.start()
            for k in block_sends(xst, xg, s_x, r_x):
                k.start()

        for k in load_gu(c):
            k.wait()
        dy = dyg.at[pl.ds(pl.multiple_of(c * rows, rows), rows)]

        for t, (start, size) in enumerate(a_tiles):
            slot = lax.rem(c * n_a + t, 2)
            load_a(t, slot).wait()
            for s, w in splits(size, 512):
                cols = pl.ds(start + s, w)
                d_hidden = nt(dy[...], wa[slot, pl.ds(s, w)])
                g, u = gb[:, cols].astype(F32), ub[:, cols].astype(F32)
                sig = jax.nn.sigmoid(g)
                silu = g * sig
                hid[pl.ds(pl.multiple_of(c * rows, rows), rows), cols] = (silu * u).astype(BF16)
                duc[:, cols] = (d_hidden * silu).astype(BF16)
                dgc[:, cols] = (d_hidden * u * (sig + silu * (1.0 - sig))).astype(BF16)
            t2 = t + 2
            if t2 < n_a:
                load_a(t2, slot).start()
            else:
                @pl.when(c < chunks - 1)
                def _():
                    load_a(t2 - n_a, slot).start()

        for k in save_d(c):
            k.start()

        @pl.when(c < chunks - 1)
        def _():
            for k in load_gu(c + 1):
                k.start()

        def part(j, carry):
            slot = lax.rem(j, 2)
            for k in load_b(j, slot):
                k.wait()

            @pl.when(j >= 2)
            def _():
                @pl.when(lax.rem(c, 2) == 0)
                def _():
                    save_f(own, j, slot).wait()

                @pl.when(lax.rem(c, 2) == 1)
                def _():
                    for k in save_b(raw_l, raw_r, j, slot):
                        k.wait()

            r = nt(dgc[...], wb[slot, 0]) + nt(duc[...], wb[slot, 1])

            @pl.when(lax.rem(c, 2) == 0)
            def _():
                st_f[slot] = r

            @pl.when(lax.rem(c, 2) == 1)
            def _():
                st_b[slot] = r.astype(BF16)

            @pl.when(c == 0)
            def _():
                save_f(own, j, slot).start()

            @pl.when(c == 2)
            def _():
                save_f(mid, j, slot).start()

            @pl.when(c == 1)
            def _():
                for k in save_b(raw_l, raw_r, j, slot):
                    k.start()

            @pl.when(c == 3)
            def _():
                for k in save_b(far_0, far_1, j, slot):
                    k.start()

            @pl.when(c * n_b + j + 2 < chunks * n_b)
            def _():
                for k in load_b(lax.rem(j + 2, n_b), slot):
                    k.start()
            return carry

        lax.fori_loop(0, n_b, part, 0)
        for slot in range(2):
            @pl.when(lax.rem(c, 2) == 0)
            def _():
                save_f(own, 0, slot).wait()

            @pl.when(lax.rem(c, 2) == 1)
            def _():
                for k in save_b(raw_l, raw_r, 0, slot):
                    k.wait()
        for k in save_d(c):
            k.wait()
        return carry

    lax.fori_loop(0, chunks, chunk, 0)

    arrived(xg, r_x, 1)
    for k in forwards(xg, s_x, r_x):
        k.start()

    def save_w(i, slot):
        at = pl.ds(pl.multiple_of(i * tm, tm), tm)
        return pltpu.make_async_copy(wa.at[slot, pl.ds(0, tm)], dwd.at[at], m_o.at[slot])

    def down(i, carry):
        slot = lax.rem(i, 2)

        @pl.when(i >= 2)
        def _():
            save_w(i, slot).wait()

        def cols(k, carry):
            at = pl.ds(pl.multiple_of(k * tn_cols, tn_cols), tn_cols)
            mine = pl.ds(pl.multiple_of(i * tm, tm), tm)
            wa[slot, pl.ds(0, tm), at] = tn(hid[:, mine], dyg[:, at]).astype(BF16)
            return carry

        lax.fori_loop(0, d // tn_cols, cols, 0)
        save_w(i, slot).start()
        return carry

    lax.fori_loop(0, ff // tm, down, 0)
    for slot in range(2):
        save_w(0, slot).wait()
    keep_x.wait()
    arrived(xg, r_x, 2)
    arrived(xg, r_x, 3)
    for k in block_sends(dy0, dyg, s_dy, r_dy) + forwards(dyg, s_dy, r_dy):
        k.wait_send()
    for k in block_sends(xst, xg, s_x, r_x) + forwards(xg, s_x, r_x):
        k.wait_send()


def weight_grad_kernel(x_ref, g_ref, o_ref):
    o_ref[...] = tn(x_ref[...], g_ref[...]).astype(BF16)


def weight_grad(x, g, tm, name):
    tokens, d = x.shape
    ff = g.shape[1]
    return pl.pallas_call(
        weight_grad_kernel, grid=(d // tm,),
        out_shape=jax.ShapeDtypeStruct((d, ff), BF16),
        in_specs=[pl.BlockSpec((tokens, tm), lambda i: (0, i)),
                  pl.BlockSpec((tokens, ff), lambda i: (0, 0), pipeline_mode=pl.Buffered(1))],
        out_specs=pl.BlockSpec((tm, ff), lambda i: (i, 0)),
        compiler_params=pltpu.CompilerParams(vmem_limit_bytes=VMEM_LIMIT),
        cost_estimate=pl.CostEstimate(flops=2 * tokens * d * ff, transcendentals=0,
                                      bytes_accessed=2 * (tokens * (d + ff) + d * ff)),
        name=name)(x, g)


def solution(mesh):
    n = mesh.shape["tp"]
    to_right = [(i, (i + 1) % n) for i in range(n)]
    to_left = [(i, (i + n - 1) % n) for i in range(n)]

    def step(x, dy, gate, up, w_gate, w_up, w_down):
        rows, d = x.shape
        tokens, ff = gate.shape
        half = rows // 2
        a_tiles, tb, tm, tn_cols = splits(ff, 1024), 512, 640, 2048
        hbm = pl.BlockSpec(memory_space=pl.ANY)

        def out(*shape, dtype=BF16):
            return jax.ShapeDtypeStruct(shape, dtype)

        ta = max(w for _, w in a_tiles)
        dma = pltpu.SemaphoreType.DMA
        xg, dg, du, own, mid, raw_l, raw_r, far_0, far_1, dwd = pl.pallas_call(
            functools.partial(gather_kernel, n, a_tiles, tb, tm, tn_cols),
            out_shape=(out(tokens, d), out(tokens, ff), out(tokens, ff), out(rows, d, dtype=F32), out(rows, d, dtype=F32),
                       out(half, d), out(half, d), out(half, d), out(half, d), out(ff, d)),
            in_specs=[hbm] * 7, out_specs=(hbm,) * 10,
            scratch_shapes=[
                pltpu.VMEM((tokens, d), BF16), pltpu.VMEM((tokens, ff), BF16),
                pltpu.VMEM((rows, ff), BF16), pltpu.VMEM((rows, ff), BF16),
                pltpu.VMEM((rows, ff), BF16), pltpu.VMEM((rows, ff), BF16),
                pltpu.VMEM((rows, d), BF16),
                pltpu.VMEM((2, ta, d), BF16), pltpu.VMEM((2, 2, tb, ff), BF16),
                pltpu.VMEM((2, rows, tb), F32), pltpu.VMEM((2, rows, tb), BF16),
                dma((4, 2)), dma((4, 2)), dma((4, 2)), dma((4, 2)),
                dma((3,)), dma((2, 2)), dma((2,)), dma((2, 2)), dma((2, 2)), dma((2,)), dma((2,)),
            ],
            compiler_params=pltpu.CompilerParams(collective_id=0, has_side_effects=True, vmem_limit_bytes=VMEM_LIMIT),
            cost_estimate=pl.CostEstimate(flops=8 * tokens * d * ff, transcendentals=tokens * ff,
                                          bytes_accessed=24 * d * ff),
            name="gather_and_rows")(dy, x, gate, up, w_down, w_gate, w_up)

        right = functools.partial(lax.ppermute, axis_name="tp", perm=to_right)
        left = functools.partial(lax.ppermute, axis_name="tp", perm=to_left)
        from_l, from_r = right(far_0), left(far_1)
        raw_from_l, raw_from_r = right(raw_r), left(raw_l)
        dw_gate = weight_grad(xg, dg, 512, "dw_gate")
        from_l, from_r, dw_gate = lax.optimization_barrier((from_l, from_r, dw_gate))
        sum_r = (mid[half:] + from_l.astype(F32)).astype(BF16)
        sum_l = (mid[:half] + from_r.astype(F32)).astype(BF16)
        sum_r, sum_l, du = lax.optimization_barrier((sum_r, sum_l, du))
        sum_from_l, sum_from_r = right(sum_r), left(sum_l)
        dw_up = weight_grad(xg, du, 512, "dw_up")
        dx = own + jnp.concatenate([sum_from_l, raw_from_l]).astype(F32) + jnp.concatenate([raw_from_r, sum_from_r]).astype(F32)
        return dx.astype(BF16), dw_gate, dw_up, dwd

    rows, cols = P(("dp", "tp"), None), P("dp", "tp")
    return jax.shard_map(
        step, mesh=mesh,
        in_specs=(rows, rows, cols, cols, P(None, "tp"), P(None, "tp"), P("tp", None)),
        out_specs=(rows, cols, cols, rows), check_vma=False)
```

time: 483 us -> 281 us (0.58); the launches traced: 475 us -> 280 us
  matrix products: 253 us -> 0 us
  Pallas kernels: 0 us -> 242 us
  waiting for transfers between devices: 116 us -> 0.02 us
  local copies, waits for them, and re-layouts: 69.9 us -> 18.2 us
  between operations: 16.6 us -> 0.67 us
  starting transfers between devices: 4.71 us -> 10.5 us
  other arithmetic: 15 us -> 9.52 us
    dot_general x7 -> x0, matrix products: 253 us -> none  [the longest x4 134 us: by_group(): jnp.einsum('gta,gtb->gab', a, b, preferred_element_type=jnp.float32)]
    pallas_call x0 -> x3, Pallas kernels: none -> 242 us  [the longest x1 172 us: step(): pl.pallas_call(functools.partial(gather_kernel, n, a_tiles, tb, tm, tn_co...]
    unnamed x5 -> x0, waiting for transfers between devices: 116 us -> none
    unnamed x10 -> x1, local copies, waits for them, and re-layouts: 69.3 us -> 18.2 us
    dot_general x1 -> x0, other arithmetic: 15 us -> none  [by_group(): jnp.einsum('gta,gtb->gab', a, b, preferred_element_type=jnp.float32)]
    ppermute x0 -> x6, starting transfers between devices: none -> 10.5 us  [the longest x2 4.07 us: step(): from_l, from_r = (right(far_0), left(far_1))]
    convert_element_type x0 -> x2, other arithmetic: none -> 9.52 us  [the longest x1 4.84 us: step(): return (dx.astype(BF16), dw_gate, dw_up, dwd)]
  transfers between devices with their start and end apart: 6 -> 6, of which waited for: 1 -> 0; matrix products, arithmetic and copies ran while one was open for 70% -> 2% of each run, Pallas kernels for 0% -> 25%
where the time goes in v1:
time: 281 us; the launch traced here: 280 us
  Pallas kernels  242 us (86%)
  local copies, waits for them, and re-layouts  18.2 us (6%)
  starting transfers between devices  10.5 us (4%)
  other arithmetic  9.52 us (3%)
    pallas_call x1, Pallas kernels, step(): pl.pallas_call(functools.partial(gather_kernel, n, a_tiles, tb, tm, tn_co...  172 us
    pallas_call x2, Pallas kernels, weight_grad(): pl.pallas_call(weight_grad_kernel, grid=(d // tm,), out_shape=jax.ShapeDt...  69.7 us
    unnamed x1, local copies, waits for them, and re-layouts  18.2 us
  transfers between devices with their start and end apart: 6, of which 0 were waited for; matrix products, arithmetic and copies ran while one was open for 2% of the time, Pallas kernels for 25%

profile of v1, /device:TPU:112, one launch (start us, length us, event | category | flops | bytes accessed | tf_op | source)
XLA Modules:
  0.0 280.5 jit_solution(18329114131368420235)
XLA Ops:
  0.6 171.8 %gather_and_rows.1 = (bf16[1024,4096]{1,0:T(8,128)(2,1)}, bf16[1024,3200]{1,0:T(8,128)(2,1)}, bf16[1024,3200]{1,0:T(8,128)(2,1)}, f32[256,4096]{1,0:T(8,128)}, f...) custom-call(bf16[256,4096]{1,0:T(8,128)(2,1)} %dy0.1, ...), custom_call_target="tpu_custom_call" | custom-call | flops 107374182400 | bytes 314572800 | tf_op jit(solution)/shard_map/gather_and_rows/pallas_call | solution.py:298
  172.5 2.4 collective-permute-start
  174.9 1.7 collective-permute-start.1
  176.5 0.4 collective-permute-start.3
  176.9 2.9 %collective-permute-start.4 = (bf16[128,4096]{1,0:T(8,128)(2,1)}, bf16[128,4096]{1,0:T(8,128)(2,1)}, u32[]{:S(2)}, u32[]{:S(2)}) collective-permute-start(bf16[128,4096]{1,0:T(8,128)(2,1)} %get-tuple-element.31), channel_id=1, source_target_pairs={{0,3},{1,0},{2,1},{3,2},{4,7},{5,4},{6,5},{7,6},{8,11},{9,8},{10,9... | collective-permute-start | bytes 3145736 | tf_op jit(solution)/shard_map/ppermute | solution.py:321
  179.8 34.9 %dw_gate.1 = bf16[4096,3200]{1,0:T(8,128)(2,1)} custom-call(bf16[1024,4096]{1,0:T(8,128)(2,1)} %get-tuple-element.24.x_ref, bf16[1024,3200]{1,0:T(8,128)(2,1)} %get-tuple-element.25.g_ref), custom_call_target="tpu_custom_call" | custom-call | flops 26843545600 | bytes 41156608 | tf_op jit(solution)/shard_map/dw_gate/pallas_call | solution.py:269
  214.6 0.0 collective-permute-done
  214.6 0.0 collective-permute-done.1
  214.7 4.7 %add_convert_fusion.1 = (bf16[128,4096]{1,0:T(8,128)(2,1)}, bf16[128,4096]{1,0:T(8,128)(2,1)}) fusion(bf16[128,4096]{1,0:T(8,128)(2,1)} %collective-permute-done.1, f32[256,4096]{1,0:T(8,128)} %get-tuple-element.21, bf16[128,4096]{1,0:T(8,128)(2,1)} %collective-permute-done), kind=kLoop, calls=%fused_computation.1 | loop fusion | flops 3145728 | bytes 8388608 | tf_op jit(solution)/shard_map/convert_element_type | solution.py:325
  219.3 0.0 collective-permute-start.2
  219.3 3.2 %collective-permute-start.5 = (bf16[128,4096]{1,0:T(8,128)(2,1)}, bf16[128,4096]{1,0:T(8,128)(2,1)}, u32[]{:S(2)}, u32[]{:S(2)}) collective-permute-start(bf16[128,4096]{1,0:T(8,128)(2,1)} %get-tuple-element.32), channel_id=1, source_target_pairs={{0,3},{1,0},{2,1},{3,2},{4,7},{5,4},{6,5},{7,6},{8,11},{9,8},{10,9... | collective-permute-start | bytes 3145736 | tf_op jit(solution)/shard_map/ppermute | solution.py:327
  222.6 34.9 %dw_up.1 = bf16[4096,3200]{1,0:T(8,128)(2,1)} custom-call(bf16[1024,4096]{1,0:T(8,128)(2,1)} %get-tuple-element.24.x_ref, bf16[1024,3200]{1,0:T(8,128)(2,1)} %get-tuple-element.34.g_ref), custom_call_target="tpu_custom_call" | custom-call | flops 26843545600 | bytes 41156608 | tf_op jit(solution)/shard_map/dw_up/pallas_call | solution.py:269
  257.4 0.0 collective-permute-done.3
  257.4 0.0 collective-permute-done.4
  257.5 0.0 collective-permute-done.2
  257.5 0.0 collective-permute-done.5
  257.5 4.8 %add_convert_fusion = bf16[256,4096]{1,0:T(8,128)(2,1)} fusion(f32[256,4096]{1,0:T(8,128)} %get-tuple-element.20, bf16[128,4096]{1,0:T(8,128)(2,1)} %collective-permute-done.3, bf16[128,4096]{1,0:T(8,128)(2,1)} %collective-permute-done.2, bf16[128,4096]{1,0:T(8,128)(2,1)} %collective-permute-done.5, bf16[128,4096]{1,0:T(8,128)(2,1)} %collective-permute-done.4), kind=kLoop, calls=%fused_computation | loop fusion | flops 11534336 | bytes 10485760 | tf_op jit(solution)/shard_map/convert_element_type | solution.py:330
  262.3 18.2 %copy.12 = bf16[3200,4096]{1,0:T(8,128)(2,1)} copy(bf16[3200,4096]{1,0:T(8,128)(2,1)} %get-tuple-element.45) | data formatting | bytes 52428800
Async XLA Ops:
  172.5 42.2 %collective-permute-start = (bf16[128,4096]{1,0:T(8,128)(2,1)}, bf16[128,4096]{1,0:T(8,128)(2,1)}, u32[]{:S(2)}, u32[]{:S(2)}) collective-permute-start(bf16[128,4096]{1,0:T(8,128)(2,1)} %get-tuple-element.22), channel_id=1, source_target_pairs={{0,1},{1,2},{2,3},{3,0},{4,5},{5,6},{6,7},{7,4},{8,9},{9,10},{10,1... | collective-permute-start | bytes 3145736 | tf_op jit(solution)/shard_map/ppermute | solution.py:320
  174.9 39.8 %collective-permute-start.1 = (bf16[128,4096]{1,0:T(8,128)(2,1)}, bf16[128,4096]{1,0:T(8,128)(2,1)}, u32[]{:S(2)}, u32[]{:S(2)}) collective-permute-start(bf16[128,4096]{1,0:T(8,128)(2,1)} %get-tuple-element.23), channel_id=1, source_target_pairs={{0,3},{1,0},{2,1},{3,2},{4,7},{5,4},{6,5},{7,6},{8,11},{9,8},{10,9... | collective-permute-start | bytes 3145736 | tf_op jit(solution)/shard_map/ppermute | solution.py:320
  176.5 80.9 %collective-permute-start.3 = (bf16[128,4096]{1,0:T(8,128)(2,1)}, bf16[128,4096]{1,0:T(8,128)(2,1)}, u32[]{:S(2)}, u32[]{:S(2)}) collective-permute-start(bf16[128,4096]{1,0:T(8,128)(2,1)} %get-tuple-element.30), channel_id=1, source_target_pairs={{0,1},{1,2},{2,3},{3,0},{4,5},{5,6},{6,7},{7,4},{8,9},{9,10},{10,1... | collective-permute-start | bytes 3145736 | tf_op jit(solution)/shard_map/ppermute | solution.py:321
  176.9 80.6 %collective-permute-start.4 = (bf16[128,4096]{1,0:T(8,128)(2,1)}, bf16[128,4096]{1,0:T(8,128)(2,1)}, u32[]{:S(2)}, u32[]{:S(2)}) collective-permute-start(bf16[128,4096]{1,0:T(8,128)(2,1)} %get-tuple-element.31), channel_id=1, source_target_pairs={{0,3},{1,0},{2,1},{3,2},{4,7},{5,4},{6,5},{7,6},{8,11},{9,8},{10,9... | collective-permute-start | bytes 3145736 | tf_op jit(solution)/shard_map/ppermute | solution.py:321
  219.3 38.1 %collective-permute-start.2 = (bf16[128,4096]{1,0:T(8,128)(2,1)}, bf16[128,4096]{1,0:T(8,128)(2,1)}, u32[]{:S(2)}, u32[]{:S(2)}) collective-permute-start(bf16[128,4096]{1,0:T(8,128)(2,1)} %get-tuple-element.29), channel_id=1, source_target_pairs={{0,1},{1,2},{2,3},{3,0},{4,5},{5,6},{6,7},{7,4},{8,9},{9,10},{10,1... | collective-permute-start | bytes 3145736 | tf_op jit(solution)/shard_map/ppermute | solution.py:327
  219.3 38.1 %collective-permute-start.5 = (bf16[128,4096]{1,0:T(8,128)(2,1)}, bf16[128,4096]{1,0:T(8,128)(2,1)}, u32[]{:S(2)}, u32[]{:S(2)}) collective-permute-start(bf16[128,4096]{1,0:T(8,128)(2,1)} %get-tuple-element.32), channel_id=1, source_target_pairs={{0,3},{1,0},{2,1},{3,2},{4,7},{5,4},{6,5},{7,6},{8,11},{9,8},{10,9... | collective-permute-start | bytes 3145736 | tf_op jit(solution)/shard_map/ppermute | solution.py:327

commit v2 on v0

v2 whole, which is shorter than its diff:
```python
import functools

import jax
import jax.numpy as jnp
from jax import lax
from jax.experimental import pallas as pl
from jax.experimental.pallas import tpu as pltpu
from jax.sharding import PartitionSpec as P


BF16, F32 = jnp.bfloat16, jnp.float32
MIB = 2**20


def nt(a, b):
    return lax.dot_general(a, b, (((1,), (1,)), ((), ())), preferred_element_type=F32)


def tn(a, b):
    return lax.dot_general(a, b, (((0,), (0,)), ((), ())), preferred_element_type=F32)


def splits(total, step):
    starts = [i * step for i in range(max(total // step, 1))]
    return [(s, e - s) for s, e in zip(starts, starts[1:] + [total])]


def rows_kernel(n, a_tiles, tb, early, dy0, x0, gate, up, w_down, w_gate, w_up,
                x_left, x_right, x_next, dyg, hid, dgu, own, mid, raw_l, raw_r, far_0, far_1,
                dyv, hv, dd, gb, wa, wb, st_f, st_b,
                s_dy, r_dy, s_x, r_x, m_in, m_gu, m_wa, m_wb, m_sf, m_sb, m_d, m_h, m_dy):
    rows, d = dy0.shape
    ff = gate.shape[1]
    half = rows // 2
    me = lax.axis_index("tp")
    right, left = lax.rem(me + 1, n), lax.rem(me + n - 1, n)
    n_a, n_b = len(a_tiles), d // tb
    chunks = 4

    def rows_of(c):
        return pl.ds(pl.multiple_of(c * rows, rows), rows)

    def place(c, p):
        return pl.ds(pl.multiple_of(c * rows + p * half, half), half)

    def tile_of(j):
        return pl.ds(pl.multiple_of(j * tb, tb), tb)

    def send(src, dst, s_sem, r_sem, c, p, to):
        return pltpu.make_async_remote_copy(src_ref=src, dst_ref=dst, send_sem=s_sem.at[c, p], recv_sem=r_sem.at[c, p],
                                            device_id={"tp": to}, device_id_type=pl.DeviceIdType.MESH)

    def block_sends(src, dsts, s_sem, r_sem):
        h0, h1 = src.at[pl.ds(0, half)], src.at[pl.ds(half, half)]
        return [send(h, dst, s_sem, r_sem, c, p, to) for (h, c, p, to), dst in
                zip(((h0, 1, 0, right), (h1, 1, 1, left), (h1, 2, 0, right), (h0, 2, 1, left)), dsts)]

    def dy_sends():
        return block_sends(dy0, [dyv.at[place(c, p)] for c in (1, 2) for p in (0, 1)], s_dy, r_dy)

    def x_sends():
        return block_sends(x0, [x_left, x_right, x_next.at[pl.ds(0, half)], x_next.at[pl.ds(half, half)]], s_x, r_x)

    def forwards():
        return [send(dyv.at[place(1, p)], dyv.at[place(3, p)], s_dy, r_dy, 3, p, to) for p, to in enumerate((right, left))]

    def load_a(t):
        start, size = a_tiles[t]
        return pltpu.make_async_copy(w_down.at[pl.ds(start, size)], wa.at[pl.ds(start, size)], m_wa.at[t])

    def load_b(j, slot):
        return [pltpu.make_async_copy(w.at[tile_of(j)], wb.at[slot, :, pl.ds(k * ff, ff)], m_wb.at[slot, k])
                for k, w in enumerate((w_gate, w_up))]

    def load_gu(c, t):
        later, last = (c + 2) // 3, c // 3
        flip = (c // 2) * (1 - last)
        first, size = a_tiles[t]
        copies = []
        for p, (shift, h) in enumerate(((later * (n - 1) - last * (n - 3), flip), (later + last, 1 - flip))):
            at = pl.ds(pl.multiple_of(lax.rem(me + shift, n) * rows + h * half, half), half)
            for k, src in enumerate((gate, up)):
                copies.append(pltpu.make_async_copy(src.at[at, pl.ds(first, size)],
                                                    gb.at[t % 2, k, pl.ds(p * half, half), pl.ds(0, size)], m_gu.at[t % 2, p, k]))
        return copies

    def save_d(c):
        k = lax.rem(c, 2)
        return pltpu.make_async_copy(dd.at[rows_of(k)], dgu.at[rows_of(c)], m_d.at[k])

    def save_h(c):
        return pltpu.make_async_copy(hv, hid.at[rows_of(c)], m_h.at[0])

    def save_dy(c):
        return pltpu.make_async_copy(dyv.at[rows_of(c)], dyg.at[rows_of(c)], m_dy.at[c])

    def save_f(dst, j):
        slot = lax.rem(j, 2)
        return pltpu.make_async_copy(st_f.at[slot], dst.at[:, tile_of(j)], m_sf.at[slot])

    def save_b(dst0, dst1, j):
        slot = lax.rem(j, 2)
        return [pltpu.make_async_copy(st_b.at[slot, pl.ds(p * half, half)], dst.at[:, tile_of(j)], m_sb.at[slot, p])
                for p, dst in enumerate((dst0, dst1))]

    def start(copies):
        for k in copies:
            k.start()

    def wait(copies):
        for k in copies:
            k.wait()

    first_dy = pltpu.make_async_copy(dy0, dyv.at[pl.ds(0, rows)], m_in.at[0])
    first_dy.start()
    load_a(0).start()
    start(load_gu(0, 0))
    load_a(1).start()
    start(load_gu(0, 1))
    for t in range(2, n_a):
        load_a(t).start()

    barrier = pltpu.get_barrier_semaphore()
    for other in (left, right):
        pl.semaphore_signal(barrier, inc=1, device_id={"tp": other}, device_id_type=pl.DeviceIdType.MESH)
    pl.semaphore_wait(barrier, 2)
    start(dy_sends())
    first_dy.wait()

    def put_f(s, j, r):
        @pl.when(s * n_b + j >= 2)
        def _():
            save_f(own, j).wait()

        st_f[lax.rem(j, 2)] = r

        @pl.when(s == 0)
        def _():
            save_f(own, j).start()

        @pl.when(s == 1)
        def _():
            save_f(mid, j).start()

    def put_b(s, j, r):
        @pl.when(s * n_b + j >= 2)
        def _():
            wait(save_b(raw_l, raw_r, j))

        st_b[lax.rem(j, 2)] = r.astype(BF16)

        @pl.when(s == 0)
        def _():
            start(save_b(raw_l, raw_r, j))

        @pl.when(s == 1)
        def _():
            start(save_b(far_0, far_1, j))

    def chunk(c, carry):
        s, k = c // 2, lax.rem(c, 2)

        @pl.when(c > 0)
        def _():
            for p in range(2):
                pltpu.make_async_copy(dyv.at[place(c, p)], dyv.at[place(c, p)], r_dy.at[c, p]).wait()

        @pl.when(c == 1)
        def _():
            start(forwards())
            start(x_sends())

        @pl.when(c >= 2)
        def _():
            save_d(c).wait()

        @pl.when(c >= 1)
        def _():
            save_h(c).wait()

        save_dy(c).start()

        dy = dyv.at[rows_of(c)]
        mine = rows_of(k)
        for t, (first, size) in enumerate(a_tiles):
            @pl.when(c == 0)
            def _():
                load_a(t).wait()

            wait(load_gu(c, t))
            cols = pl.ds(first, size)
            d_hidden = nt(dy[...], wa[cols])
            g, u = (gb[t % 2, m, :, pl.ds(0, size)].astype(F32) for m in range(2))
            sig = jax.nn.sigmoid(g)
            silu = g * sig
            hv[:, cols] = (silu * u).astype(BF16)
            dd[mine, pl.ds(ff + first, size)] = (d_hidden * silu).astype(BF16)
            dd[mine, cols] = (d_hidden * u * (sig + silu * (1.0 - sig))).astype(BF16)
            if t + 2 < n_a:
                start(load_gu(c, t + 2))
            else:
                @pl.when(c < chunks - 1)
                def _():
                    start(load_gu(c + 1, t + 2 - n_a))
            if t == 1:
                @pl.when(c == 0)
                def _():
                    start(load_b(0, 0) + load_b(1, 1))

        save_d(c).start()
        save_h(c).start()

        def next_b(i):
            i2 = i + 2
            wrap = i2 // (early + n_b)

            @pl.when(s + wrap < 2)
            def _():
                i3 = i2 - wrap * (early + n_b)
                late = jnp.minimum(i3 // (2 * early), 1)
                start(load_b(lax.rem(i3, early) * (1 - late) + (i3 - early) * late, lax.rem(i, 2)))

        def one(j, carry):
            i = k * early + j
            slot = lax.rem(i, 2)
            wait(load_b(j, slot))
            r = nt(dd[mine, :], wb[slot])

            @pl.when(k == 0)
            def _():
                put_f(s, j, r)

            @pl.when(k == 1)
            def _():
                put_b(s, j, r)

            next_b(i)
            return carry

        lax.fori_loop(0, early, one, 0)

        def both(j, carry):
            i = early + j
            slot = lax.rem(i, 2)
            wait(load_b(j, slot))
            r = nt(dd[...], wb[slot])
            put_f(s, j, r[:rows])
            put_b(s, j, r[rows:])
            next_b(i)
            return carry

        lax.fori_loop(early, early + k * (n_b - early), both, 0)
        return carry

    lax.fori_loop(0, chunks, chunk, 0)

    for j in range(2):
        save_f(own, j).wait()
        wait(save_b(raw_l, raw_r, j))
        save_d(j).wait()
    save_h(0).wait()
    for c in range(chunks):
        save_dy(c).wait()
    for k in dy_sends() + forwards() + x_sends():
        k.wait_send()
    for k in x_sends():
        k.wait_recv()


def down_kernel(h_ref, dy_ref, o_ref):
    o_ref[...] = tn(h_ref[...], dy_ref[...]).astype(BF16)


def down_grad(hid, dyg, tm):
    tokens, ff = hid.shape
    d = dyg.shape[1]
    return pl.pallas_call(
        down_kernel, grid=(ff // tm,),
        out_shape=jax.ShapeDtypeStruct((ff, d), BF16),
        in_specs=[pl.BlockSpec((tokens, tm), lambda i: (0, i)),
                  pl.BlockSpec((tokens, d), lambda i: (0, 0), pipeline_mode=pl.Buffered(1))],
        out_specs=pl.BlockSpec((tm, d), lambda i: (i, 0)),
        compiler_params=pltpu.CompilerParams(vmem_limit_bytes=DOWN_MIB * MIB),
        cost_estimate=pl.CostEstimate(flops=2 * tokens * d * ff, transcendentals=0,
                                      bytes_accessed=2 * (tokens * (d + ff) + d * ff)),
        name="dw_down")(hid, dyg)


def gate_up_kernel(ff, n_x, *refs):
    x = jnp.concatenate([r[...] for r in refs[:n_x]], axis=0)
    o_gate, o_up = refs[-2:]
    r = tn(x, refs[n_x][...])
    o_gate[...] = r[:, :ff].astype(BF16)
    o_up[...] = r[:, ff:].astype(BF16)


def gate_up_grad(xs, dgu, tm, first, steps, earlier):
    tokens, ff2 = dgu.shape
    d, ff = xs[0].shape[1], ff2 // 2
    out = jax.ShapeDtypeStruct((d, ff), BF16)
    spec = pl.BlockSpec((tm, ff), lambda i: (i + first, 0))
    n_x = len(xs)
    return pl.pallas_call(
        functools.partial(gate_up_kernel, ff, n_x), grid=(steps,), out_shape=(out, out),
        in_specs=[pl.BlockSpec((x.shape[0], tm), lambda i: (0, i + first)) for x in xs]
        + [pl.BlockSpec((tokens, ff2), lambda i: (0, 0), pipeline_mode=pl.Buffered(1))]
        + [pl.BlockSpec(memory_space=pl.ANY)] * len(earlier),
        out_specs=(spec, spec),
        input_output_aliases={n_x + 1 + k: k for k in range(len(earlier))},
        compiler_params=pltpu.CompilerParams(vmem_limit_bytes=GU_MIB * MIB),
        cost_estimate=pl.CostEstimate(flops=2 * tokens * tm * steps * ff2, transcendentals=0,
                                      bytes_accessed=2 * (tokens * (tm * steps + ff2) + tm * steps * ff2)),
        name="dw_gate_up")(*xs, dgu, *earlier)


DOWN_MIB, GU_MIB = 40, 34


def solution(mesh):
    n = mesh.shape["tp"]
    to_right = [(i, (i + 1) % n) for i in range(n)]
    to_left = [(i, (i + n - 1) % n) for i in range(n)]

    def step(x, dy, gate, up, w_gate, w_up, w_down):
        rows, d = x.shape
        tokens, ff = gate.shape
        half = rows // 2
        a_tiles, tb, early, tm, td = splits(ff, 768), 512, 2, 256, 640
        hbm = pl.BlockSpec(memory_space=pl.ANY)

        def out(*shape, dtype=BF16):
            return jax.ShapeDtypeStruct(shape, dtype)

        ta = max(w for _, w in a_tiles)
        assert len(a_tiles) % 2 == 0 and early % 2 == 0
        dma, vmem = pltpu.SemaphoreType.DMA, pltpu.VMEM
        x_left, x_right, x_next, dyg, hid, dgu, own, mid, raw_l, raw_r, far_0, far_1 = pl.pallas_call(
            functools.partial(rows_kernel, n, a_tiles, tb, early),
            out_shape=(out(half, d), out(half, d), out(rows, d), out(tokens, d), out(tokens, ff), out(tokens, 2 * ff),
                       out(rows, d, dtype=F32), out(rows, d, dtype=F32),
                       out(half, d), out(half, d), out(half, d), out(half, d)),
            in_specs=[hbm] * 7, out_specs=(hbm,) * 12,
            scratch_shapes=[
                vmem((tokens, d), BF16), vmem((rows, ff), BF16), vmem((2 * rows, 2 * ff), BF16),
                vmem((2, 2, rows, ta), BF16), vmem((ff, d), BF16), vmem((2, tb, 2 * ff), BF16),
                vmem((2, rows, tb), F32), vmem((2, rows, tb), BF16),
                dma((4, 2)), dma((4, 2)), dma((3, 2)), dma((3, 2)),
                dma((1,)), dma((2, 2, 2)), dma((len(a_tiles),)), dma((2, 2)), dma((2,)), dma((2, 2)), dma((2,)), dma((1,)), dma((4,)),
            ],
            compiler_params=pltpu.CompilerParams(collective_id=0, has_side_effects=True, vmem_limit_bytes=67_000_000),
            cost_estimate=pl.CostEstimate(flops=6 * tokens * d * ff, transcendentals=tokens * ff,
                                          bytes_accessed=16 * d * ff),
            name="rows")(dy, x, gate, up, w_down, w_gate, w_up)

        def hop(array, to):
            return lax.ppermute(array, "tp", to)

        x_far_0, x_far_1 = hop(x_left, to_right), hop(x_right, to_left)
        from_l, from_r = hop(far_0, to_right), hop(far_1, to_left)
        raw_from_l, raw_from_r = hop(raw_r, to_right), hop(raw_l, to_left)
        dw_down = down_grad(hid, dyg, td)
        x_far_0, x_far_1, dw_down = lax.optimization_barrier((x_far_0, x_far_1, dw_down))
        xs = (x, x_left, x_right, x_next, x_far_0, x_far_1)
        steps = d // tm
        cut = steps // 2
        dw = gate_up_grad(xs, dgu, tm, 0, cut, ())
        from_l, from_r, dw = lax.optimization_barrier((from_l, from_r, dw))
        sum_r = (mid[half:] + from_l.astype(F32)).astype(BF16)
        sum_l = (mid[:half] + from_r.astype(F32)).astype(BF16)
        sum_r, sum_l, dw = lax.optimization_barrier((sum_r, sum_l, dw))
        sum_from_l, sum_from_r = hop(sum_r, to_right), hop(sum_l, to_left)
        dw_gate, dw_up = gate_up_grad(xs, dgu, tm, cut, steps - cut, dw)
        dx = own + jnp.concatenate([sum_from_l, raw_from_l]).astype(F32) + jnp.concatenate([raw_from_r, sum_from_r]).astype(F32)
        return dx.astype(BF16), dw_gate, dw_up, dw_down

    rows, cols = P(("dp", "tp"), None), P("dp", "tp")
    return jax.shard_map(
        step, mesh=mesh,
        in_specs=(rows, rows, cols, cols, P(None, "tp"), P(None, "tp"), P("tp", None)),
        out_specs=(rows, cols, cols, rows), check_vma=False)
```

time: 483 us -> 268 us (0.55); the launches traced: 475 us -> 268 us
  matrix products: 253 us -> 0 us
  Pallas kernels: 0 us -> 224 us
  waiting for transfers between devices: 116 us -> 26.3 us
  local copies, waits for them, and re-layouts: 69.9 us -> 2.89 us
  between operations: 16.6 us -> 0.74 us
  other arithmetic: 15 us -> 2.57 us
  starting transfers between devices: 4.71 us -> 11.3 us
    dot_general x7 -> x0, matrix products: 253 us -> none  [the longest x4 134 us: by_group(): jnp.einsum('gta,gtb->gab', a, b, preferred_element_type=jnp.float32)]
    pallas_call x0 -> x4, Pallas kernels: none -> 224 us  [the longest x1 118 us: step(): pl.pallas_call(functools.partial(rows_kernel, n, a_tiles, tb, early), out...]
    unnamed x5 -> x0, waiting for transfers between devices: 116 us -> none
    unnamed x10 -> x16, local copies, waits for them, and re-layouts: 69.3 us -> 2.89 us
    ppermute x0 -> x8, waiting for transfers between devices: none -> 26.3 us  [hop(): return lax.ppermute(array, 'tp', to)]
    dot_general x1 -> x0, other arithmetic: 15 us -> none  [by_group(): jnp.einsum('gta,gtb->gab', a, b, preferred_element_type=jnp.float32)]
    ppermute x0 -> x8, starting transfers between devices: none -> 11.3 us  [hop(): return lax.ppermute(array, 'tp', to)]
  transfers between devices with their start and end apart: 6 -> 8, of which waited for: 1 -> 1; matrix products, arithmetic and copies ran while one was open for 70% -> 0% of each run, Pallas kernels for 0% -> 39%
where the time goes in v2:
time: 268 us
  Pallas kernels  224 us (84%)
  waiting for transfers between devices  26.3 us (10%)
  starting transfers between devices  11.3 us (4%)
  local copies, waits for them, and re-layouts  2.89 us (1%)
    pallas_call x1, Pallas kernels, step(): pl.pallas_call(functools.partial(rows_kernel, n, a_tiles, tb, early), out...  118 us
    pallas_call x2, Pallas kernels, gate_up_grad(): pl.pallas_call(functools.partial(gate_up_kernel, ff, n_x), grid=(steps,),...  71 us
    pallas_call x1, Pallas kernels, down_grad(): pl.pallas_call(down_kernel, grid=(ff // tm,), out_shape=jax.ShapeDtypeStr...  34.7 us
    ppermute x8, waiting for transfers between devices, hop(): return lax.ppermute(array, 'tp', to)  26.3 us
    ppermute x8, starting transfers between devices, hop(): return lax.ppermute(array, 'tp', to)  11.3 us
  transfers between devices with their start and end apart: 8, of which 1 were waited for; matrix products, arithmetic and copies ran while one was open for 0% of the time, Pallas kernels for 39%

profile of v2, /device:TPU:112, one launch (start us, length us, event | category | flops | bytes accessed | tf_op | source)
XLA Modules:
  0.0 267.8 jit_solution(16168285937068826825)
XLA Ops:
  0.6 118.3 %rows.1 = (bf16[128,4096]{1,0:T(8,128)(2,1)}, bf16[128,4096]{1,0:T(8,128)(2,1)}, bf16[256,4096]{1,0:T(8,128)(2,1)}, bf16[1024,4096]{1,0:T(8,128)(2,1)}, bf16[102...) custom-call(bf16[256,4096]{1,0:T(8,128)(2,1)} %dy0.1, ...), custom_call_target="tpu_custom_call" | custom-call | flops 80530636800 | bytes 209715200 | tf_op jit(solution)/shard_map/rows/pallas_call | solution.py:337
  119.0 1.4 collective-permute-start
  120.4 1.9 collective-permute-start.1
  122.3 0.1 collective-permute-start.5
  122.4 0.6 collective-permute-start.2
  123.0 2.6 collective-permute-start.3
  125.6 0.0 copy-start.4
  125.6 2.9 %copy-done.4 = bf16[1024,3200]{1,0:T(8,128)(2,1)S(1)} copy-done((bf16[1024,3200]{1,0:T(8,128)(2,1)S(1)}, bf16[1024,3200]{1,0:T(8,128)(2,1)}, u32[]{:S(2)}) %copy-start.4) | copy-done | bytes 6553624
  128.5 0.0 copy-start.7
  128.5 0.0 copy-start
  128.5 0.0 copy-start.1
  128.5 0.0 copy-start.2
  128.5 0.0 copy-start.3
  128.5 34.7 %dw_down.1 = bf16[3200,4096]{1,0:T(8,128)(2,1)} custom-call(bf16[1024,3200]{1,0:T(8,128)(2,1)S(1)} %copy-done.4, bf16[1024,4096]{1,0:T(8,128)(2,1)} %get-tuple-element.39.dy_ref), custom_call_target="tpu_custom_call" | custom-call | flops 26843545600 | bytes 41156608 | tf_op jit(solution)/shard_map/dw_down/pallas_call | solution.py:277
  163.2 26.3 %collective-permute-done.2.refs_4_ = bf16[128,4096]{1,0:T(8,128)(2,1)S(1)} collective-permute-done((bf16[128,4096]{1,0:T(8,128)(2,1)}, bf16[128,4096]{1,0:T(8,128)(2,1)S(1)}, u32[]{:S(2)}, u32[]{:S(2)}) %collective-permute-start.2) | collective-permute-done | bytes 1048608 | tf_op jit(solution)/shard_map/ppermute | solution.py:356
  189.5 0.0 copy-done.7
  189.5 1.3 collective-permute-start.6
  190.9 0.0 collective-permute-done.3.refs_5_
  190.9 0.0 copy-done
  190.9 0.0 copy-done.1
  190.9 0.0 copy-done.2
  190.9 0.0 copy-done.3
  190.9 0.0 copy-start.6
  190.9 35.6 %dw_gate_up.2 = (bf16[4096,3200]{1,0:T(8,128)(2,1)}, bf16[4096,3200]{1,0:T(8,128)(2,1)}) custom-call(bf16[256,4096]{1,0:T(8,128)(2,1)S(1)} %copy-done, bf16[128,4096]{1,0:T(8,128)(2,1)S(1)} %copy-done.1, bf16[128,4096]{1,0:T(8,128)(2,1)S(1)} %copy-done.2, bf16[256,4096]{1,0:T(8,128)(2,1)S(1)} %copy-done.3, ...), custom_call_target="tpu_custom_call" | custom-call | flops 26843545600 | bytes 43515904 | tf_op jit(solution)/shard_map/dw_gate_up/pallas_call | solution.py:303
  226.5 0.0 collective-permute-done
  226.5 0.0 collective-permute-done.1
  226.5 0.0 copy-done.6
  226.5 0.6 add_convert_fusion.1
  227.0 0.0 copy-start.5
  227.1 0.8 collective-permute-start.4
  227.8 2.5 collective-permute-start.7
  230.4 35.4 %dw_gate_up.3 = (bf16[4096,3200]{1,0:T(8,128)(2,1)}, bf16[4096,3200]{1,0:T(8,128)(2,1)}) custom-call(bf16[256,4096]{1,0:T(8,128)(2,1)S(1)} %copy-done, bf16[128,4096]{1,0:T(8,128)(2,1)S(1)} %copy-done.1, bf16[128,4096]{1,0:T(8,128)(2,1)S(1)} %copy-done.2, bf16[256,4096]{1,0:T(8,128)(2,1)S(1)} %copy-done.3, ...), custom_call_target="tpu_custom_call", output_to_operand_aliasing={{0}: (7, {}), {1}: (8, {})} | custom-call | flops 26843545600 | bytes 43515904 | tf_op jit(solution)/shard_map/dw_gate_up/pallas_call | solution.py:303
  265.8 0.0 collective-permute-done.5
  265.8 0.0 collective-permute-done.6
  265.8 0.0 collective-permute-done.4
  265.8 0.0 collective-permute-done.7
  265.8 0.0 copy-done.5
  265.8 2.0 add_convert_fusion
Async XLA Ops:
  119.0 107.5 %collective-permute-start = (bf16[128,4096]{1,0:T(8,128)(2,1)}, bf16[128,4096]{1,0:T(8,128)(2,1)S(1)}, u32[]{:S(2)}, u32[]{:S(2)}) collective-permute-start(bf16[128,4096]{1,0:T(8,128)(2,1)} %get-tuple-element.33), channel_id=1, source_target_pairs={{0,1},{1,2},{2,3},{3,0},{4,5},{5,6},{6,7},{7,4},{8,9},{9,10},{10,1... | collective-permute-start | bytes 3145736 | tf_op jit(solution)/shard_map/ppermute | solution.py:356
  120.4 106.1 %collective-permute-start.1 = (bf16[128,4096]{1,0:T(8,128)(2,1)}, bf16[128,4096]{1,0:T(8,128)(2,1)S(1)}, u32[]{:S(2)}, u32[]{:S(2)}) collective-permute-start(bf16[128,4096]{1,0:T(8,128)(2,1)} %get-tuple-element.34), channel_id=1, source_target_pairs={{0,3},{1,0},{2,1},{3,2},{4,7},{5,4},{6,5},{7,6},{8,11},{9,8},{10,9... | collective-permute-start | bytes 3145736 | tf_op jit(solution)/shard_map/ppermute | solution.py:356
  122.3 143.5 %collective-permute-start.5 = (bf16[128,4096]{1,0:T(8,128)(2,1)}, bf16[128,4096]{1,0:T(8,128)(2,1)S(1)}, u32[]{:S(2)}, u32[]{:S(2)}) collective-permute-start(bf16[128,4096]{1,0:T(8,128)(2,1)} %get-tuple-element.50), channel_id=1, source_target_pairs={{0,1},{1,2},{2,3},{3,0},{4,5},{5,6},{6,7},{7,4},{8,9},{9,10},{10,1... | collective-permute-start | bytes 3145736 | tf_op jit(solution)/shard_map/ppermute | solution.py:356
  122.4 67.1 %collective-permute-start.2 = (bf16[128,4096]{1,0:T(8,128)(2,1)}, bf16[128,4096]{1,0:T(8,128)(2,1)S(1)}, u32[]{:S(2)}, u32[]{:S(2)}) collective-permute-start(bf16[128,4096]{1,0:T(8,128)(2,1)} %get-tuple-element.35.refs_1_), channel_id=1, source_target_pairs={{0,1},{1,2},{2,3},{3,0},{4,5},{5,6},{6,7},{7,4},{8,9},{9,10},{10,1... | collective-permute-start | bytes 3145736 | tf_op jit(solution)/shard_map/ppermute | solution.py:356
  123.0 67.8 %collective-permute-start.3 = (bf16[128,4096]{1,0:T(8,128)(2,1)}, bf16[128,4096]{1,0:T(8,128)(2,1)S(1)}, u32[]{:S(2)}, u32[]{:S(2)}) collective-permute-start(bf16[128,4096]{1,0:T(8,128)(2,1)} %get-tuple-element.36.refs_2_), channel_id=1, source_target_pairs={{0,3},{1,0},{2,1},{3,2},{4,7},{5,4},{6,5},{7,6},{8,11},{9,8},{10,9... | collective-permute-start | bytes 3145736 | tf_op jit(solution)/shard_map/ppermute | solution.py:356
  125.6 2.9 %copy-start.4 = (bf16[1024,3200]{1,0:T(8,128)(2,1)S(1)}, bf16[1024,3200]{1,0:T(8,128)(2,1)}, u32[]{:S(2)}) copy-start(bf16[1024,3200]{1,0:T(8,128)(2,1)} %get-tuple-element.38.h_ref) | copy-start | bytes 19660804
  128.5 61.0 %copy-start.7 = (bf16[128,4096]{1,0:T(8,128)(2,1)S(1)}, bf16[128,4096]{1,0:T(8,128)(2,1)}, u32[]{:S(2)}) copy-start(bf16[128,4096]{1,0:T(8,128)(2,1)} %get-tuple-element.51) | copy-start | bytes 3145732
  128.5 62.4 %copy-start = (bf16[256,4096]{1,0:T(8,128)(2,1)S(1)}, bf16[256,4096]{1,0:T(8,128)(2,1)}, u32[]{:S(2)}) copy-start(bf16[256,4096]{1,0:T(8,128)(2,1)} %refs_0_.3) | copy-start | bytes 6291460
  128.5 62.4 %copy-start.1 = (bf16[128,4096]{1,0:T(8,128)(2,1)S(1)}, bf16[128,4096]{1,0:T(8,128)(2,1)}, u32[]{:S(2)}) copy-start(bf16[128,4096]{1,0:T(8,128)(2,1)} %get-tuple-element.35.refs_1_) | copy-start | bytes 3145732
  128.5 62.4 %copy-start.2 = (bf16[128,4096]{1,0:T(8,128)(2,1)S(1)}, bf16[128,4096]{1,0:T(8,128)(2,1)}, u32[]{:S(2)}) copy-start(bf16[128,4096]{1,0:T(8,128)(2,1)} %get-tuple-element.36.refs_2_) | copy-start | bytes 3145732
  128.5 62.4 %copy-start.3 = (bf16[256,4096]{1,0:T(8,128)(2,1)S(1)}, bf16[256,4096]{1,0:T(8,128)(2,1)}, u32[]{:S(2)}) copy-start(bf16[256,4096]{1,0:T(8,128)(2,1)} %get-tuple-element.37.refs_3_) | copy-start | bytes 6291460
  189.5 76.3 %collective-permute-start.6 = (bf16[128,4096]{1,0:T(8,128)(2,1)S(1)}, bf16[128,4096]{1,0:T(8,128)(2,1)S(1)}, u32[]{:S(2)}, u32[]{:S(2)}) collective-permute-start(bf16[128,4096]{1,0:T(8,128)(2,1)S(1)} %copy-done.7), channel_id=1, source_target_pairs={{0,3},{1,0},{2,1},{3,2},{4,7},{5,4},{6,5},{7,6},{8,11},{9,8},{10,9... | collective-permute-start | bytes 3145736 | tf_op jit(solution)/shard_map/ppermute | solution.py:356
  190.9 35.6 %copy-start.6 = (f32[256,4096]{1,0:T(8,128)S(1)}, f32[256,4096]{1,0:T(8,128)}, u32[]{:S(2)}) copy-start(f32[256,4096]{1,0:T(8,128)} %get-tuple-element.32) | copy-start | bytes 12582916
  227.0 38.8 %copy-start.5 = (f32[256,4096]{1,0:T(8,128)S(1)}, f32[256,4096]{1,0:T(8,128)}, u32[]{:S(2)}) copy-start(f32[256,4096]{1,0:T(8,128)} %get-tuple-element.31) | copy-start | bytes 12582916
  227.1 38.7 %collective-permute-start.4 = (bf16[128,4096]{1,0:T(8,128)(2,1)S(1)}, bf16[128,4096]{1,0:T(8,128)(2,1)S(1)}, u32[]{:S(2)}, u32[]{:S(2)}) collective-permute-start(bf16[128,4096]{1,0:T(8,128)(2,1)S(1)} %get-tuple-element.49), channel_id=1, source_target_pairs={{0,1},{1,2},{2,3},{3,0},{4,5},{5,6},{6,7},{7,4},{8,9},{9,10},{10,1... | collective-permute-start | bytes 3145736 | tf_op jit(solution)/shard_map/ppermute | solution.py:356
  227.8 38.0 %collective-permute-start.7 = (bf16[128,4096]{1,0:T(8,128)(2,1)S(1)}, bf16[128,4096]{1,0:T(8,128)(2,1)S(1)}, u32[]{:S(2)}, u32[]{:S(2)}) collective-permute-start(bf16[128,4096]{1,0:T(8,128)(2,1)S(1)} %get-tuple-element.52), channel_id=1, source_target_pairs={{0,3},{1,0},{2,1},{3,2},{4,7},{5,4},{6,5},{7,6},{8,11},{9,8},{10,9... | collective-permute-start | bytes 3145736 | tf_op jit(solution)/shard_map/ppermute | solution.py:356

commit v3 on v2

--- a/solution.py
+++ b/solution.py
@@ -26,7 +26,7 @@
 
 
 def rows_kernel(n, a_tiles, tb, early, dy0, x0, gate, up, w_down, w_gate, w_up,
-                x_left, x_right, x_next, dyg, hid, dgu, own, mid, raw_l, raw_r, far_0, far_1,
+                x_left, x_right, x_next, dyg, hid, dgu, own, mid, out_r, out_l,
                 dyv, hv, dd, gb, wa, wb, st_f, st_b,
                 s_dy, r_dy, s_x, r_x, m_in, m_gu, m_wa, m_wb, m_sf, m_sb, m_d, m_h, m_dy):
     rows, d = dy0.shape
@@ -98,10 +98,12 @@
         slot = lax.rem(j, 2)
         return pltpu.make_async_copy(st_f.at[slot], dst.at[:, tile_of(j)], m_sf.at[slot])
 
-    def save_b(dst0, dst1, j):
+    def save_b(near, j):
         slot = lax.rem(j, 2)
-        return [pltpu.make_async_copy(st_b.at[slot, pl.ds(p * half, half)], dst.at[:, tile_of(j)], m_sb.at[slot, p])
-                for p, dst in enumerate((dst0, dst1))]
+        dsts = (out_l, out_r) if near else (out_r, out_l)
+        return [pltpu.make_async_copy(st_b.at[slot, pl.ds(p * half, half)],
+                                      dst.at[pl.ds(half if near else 0, half), tile_of(j)], m_sb.at[slot, p])
+                for p, dst in enumerate(dsts)]
 
     def start(copies):
         for k in copies:
@@ -145,17 +147,17 @@
     def put_b(s, j, r):
         @pl.when(s * n_b + j >= 2)
         def _():
-            wait(save_b(raw_l, raw_r, j))
+            wait(save_b(True, j))
 
         st_b[lax.rem(j, 2)] = r.astype(BF16)
 
         @pl.when(s == 0)
         def _():
-            start(save_b(raw_l, raw_r, j))
+            start(save_b(True, j))
 
         @pl.when(s == 1)
         def _():
-            start(save_b(far_0, far_1, j))
+            start(save_b(False, j))
 
     def chunk(c, carry):
         s, k = c // 2, lax.rem(c, 2)
@@ -256,7 +258,7 @@
 
     for j in range(2):
         save_f(own, j).wait()
-        wait(save_b(raw_l, raw_r, j))
+        wait(save_b(True, j))
         save_d(j).wait()
     save_h(0).wait()
     for c in range(chunks):
@@ -313,7 +315,7 @@
         name="dw_gate_up")(*xs, dgu, *earlier)
 
 
-DOWN_MIB, GU_MIB = 40, 34
+DOWN_MIB, GU_MIB = 28, 24
 
 
 def solution(mesh):
@@ -334,12 +336,12 @@
         ta = max(w for _, w in a_tiles)
         assert len(a_tiles) % 2 == 0 and early % 2 == 0
         dma, vmem = pltpu.SemaphoreType.DMA, pltpu.VMEM
-        x_left, x_right, x_next, dyg, hid, dgu, own, mid, raw_l, raw_r, far_0, far_1 = pl.pallas_call(
+        x_left, x_right, x_next, dyg, hid, dgu, own, mid, out_r, out_l = pl.pallas_call(
             functools.partial(rows_kernel, n, a_tiles, tb, early),
             out_shape=(out(half, d), out(half, d), out(rows, d), out(tokens, d), out(tokens, ff), out(tokens, 2 * ff),
                        out(rows, d, dtype=F32), out(rows, d, dtype=F32),
-                       out(half, d), out(half, d), out(half, d), out(half, d)),
-            in_specs=[hbm] * 7, out_specs=(hbm,) * 12,
+                       out(rows, d), out(rows, d)),
+            in_specs=[hbm] * 7, out_specs=(hbm,) * 10,
             scratch_shapes=[
                 vmem((tokens, d), BF16), vmem((rows, ff), BF16), vmem((2 * rows, 2 * ff), BF16),
                 vmem((2, 2, rows, ta), BF16), vmem((ff, d), BF16), vmem((2, tb, 2 * ff), BF16),
@@ -356,8 +358,7 @@
             return lax.ppermute(array, "tp", to)
 
         x_far_0, x_far_1 = hop(x_left, to_right), hop(x_right, to_left)
-        from_l, from_r = hop(far_0, to_right), hop(far_1, to_left)
-        raw_from_l, raw_from_r = hop(raw_r, to_right), hop(raw_l, to_left)
+        from_l, from_r = hop(out_r, to_right), hop(out_l, to_left)
         dw_down = down_grad(hid, dyg, td)
         x_far_0, x_far_1, dw_down = lax.optimization_barrier((x_far_0, x_far_1, dw_down))
         xs = (x, x_left, x_right, x_next, x_far_0, x_far_1)
@@ -365,13 +366,15 @@
         cut = steps // 2
         dw = gate_up_grad(xs, dgu, tm, 0, cut, ())
         from_l, from_r, dw = lax.optimization_barrier((from_l, from_r, dw))
-        sum_r = (mid[half:] + from_l.astype(F32)).astype(BF16)
-        sum_l = (mid[:half] + from_r.astype(F32)).astype(BF16)
+        sum_r = (mid[half:] + from_l[:half].astype(F32)).astype(BF16)
+        sum_l = (mid[:half] + from_r[:half].astype(F32)).astype(BF16)
         sum_r, sum_l, dw = lax.optimization_barrier((sum_r, sum_l, dw))
         sum_from_l, sum_from_r = hop(sum_r, to_right), hop(sum_l, to_left)
         dw_gate, dw_up = gate_up_grad(xs, dgu, tm, cut, steps - cut, dw)
-        dx = own + jnp.concatenate([sum_from_l, raw_from_l]).astype(F32) + jnp.concatenate([raw_from_r, sum_from_r]).astype(F32)
-        return dx.astype(BF16), dw_gate, dw_up, dw_down
+        top = own[:half] + sum_from_l.astype(F32) + from_r[half:].astype(F32)
+        bottom = own[half:] + from_l[half:].astype(F32) + sum_from_r.astype(F32)
+        dx = jnp.concatenate([top.astype(BF16), bottom.astype(BF16)])
+        return dx, dw_gate, dw_up, dw_down
 
     rows, cols = P(("dp", "tp"), None), P("dp", "tp")
     return jax.shard_map(

time: 268 us -> 234 us (0.87)
  waiting for transfers between devices: 26.3 us -> 0.02 us
  Pallas kernels: 224 us -> 211 us
  other arithmetic: 2.57 us -> 6.15 us
  local copies, waits for them, and re-layouts: 2.89 us -> 6.27 us
    ppermute x8 -> x6, waiting for transfers between devices: 26.3 us -> 0.02 us  [hop(): return lax.ppermute(array, 'tp', to)]
    pallas_call x2, Pallas kernels: 71 us -> 61.5 us  [gate_up_grad(): pl.pallas_call(functools.partial(gate_up_kernel, ff, n_x), grid=(steps,),...]
    pallas_call x1, Pallas kernels: 34.7 us -> 31.2 us  [down_grad(): pl.pallas_call(down_kernel, grid=(ff // tm,), out_shape=jax.ShapeDtypeStr...]
    unnamed x16 -> x18, local copies, waits for them, and re-layouts: 2.89 us -> 6.27 us
    ppermute x8 -> x6, starting transfers between devices: 11.3 us -> 9.86 us  [hop(): return lax.ppermute(array, 'tp', to)]
  transfers between devices with their start and end apart: 8 -> 6, of which waited for: 1 -> 0; matrix products, arithmetic and copies ran while one was open for 0% -> 0% of each run, Pallas kernels for 39% -> 40%
where the time goes in v3:
time: 234 us
  Pallas kernels  211 us (90%)
  starting transfers between devices  9.86 us (4%)
  local copies, waits for them, and re-layouts  6.27 us (3%)
  other arithmetic  6.15 us (3%)
    pallas_call x1, Pallas kernels, step(): pl.pallas_call(functools.partial(rows_kernel, n, a_tiles, tb, early), out...  118 us
    pallas_call x2, Pallas kernels, gate_up_grad(): pl.pallas_call(functools.partial(gate_up_kernel, ff, n_x), grid=(steps,),...  61.5 us
    pallas_call x1, Pallas kernels, down_grad(): pl.pallas_call(down_kernel, grid=(ff // tm,), out_shape=jax.ShapeDtypeStr...  31.2 us
    ppermute x6, starting transfers between devices, hop(): return lax.ppermute(array, 'tp', to)  9.86 us
    unnamed x18, local copies, waits for them, and re-layouts  6.27 us
  transfers between devices with their start and end apart: 6, of which 0 were waited for; matrix products, arithmetic and copies ran while one was open for 0% of the time, Pallas kernels for 40%

profile of v3, /device:TPU:112, one launch (start us, length us, event | category | flops | bytes accessed | tf_op | source)
XLA Modules:
  0.0 234.1 jit_solution(17329988607383927990)
XLA Ops:
  0.6 118.3 %rows.1 = (bf16[128,4096]{1,0:T(8,128)(2,1)}, bf16[128,4096]{1,0:T(8,128)(2,1)}, bf16[256,4096]{1,0:T(8,128)(2,1)}, bf16[1024,4096]{1,0:T(8,128)(2,1)}, bf16[102...) custom-call(bf16[256,4096]{1,0:T(8,128)(2,1)} %dy0.1, ...), custom_call_target="tpu_custom_call" | custom-call | flops 80530636800 | bytes 209715200 | tf_op jit(solution)/shard_map/rows/pallas_call | solution.py:339
  119.0 1.4 collective-permute-start.2
  120.4 1.9 collective-permute-start.3
  122.3 0.1 collective-permute-start
  122.4 3.1 %collective-permute-start.1 = (bf16[256,4096]{1,0:T(8,128)(2,1)}, bf16[256,4096]{1,0:T(8,128)(2,1)}, u32[]{:S(2)}, u32[]{:S(2)}) collective-permute-start(bf16[256,4096]{1,0:T(8,128)(2,1)} %get-tuple-element.32), channel_id=1, source_target_pairs={{0,3},{1,0},{2,1},{3,2},{4,7},{5,4},{6,5},{7,6},{8,11},{9,8},{10,9... | collective-permute-start | bytes 6291464 | tf_op jit(solution)/shard_map/ppermute | solution.py:358
  125.5 0.0 copy-start.5
  125.5 3.4 %copy-done.5 = bf16[1024,4096]{1,0:T(8,128)(2,1)S(1)} copy-done((bf16[1024,4096]{1,0:T(8,128)(2,1)S(1)}, bf16[1024,4096]{1,0:T(8,128)(2,1)}, u32[]{:S(2)}) %copy-start.5) | copy-done | bytes 8388632
  128.9 0.0 copy-start.6
  128.9 2.9 %copy-done.6 = bf16[1024,3200]{1,0:T(8,128)(2,1)S(1)} copy-done((bf16[1024,3200]{1,0:T(8,128)(2,1)S(1)}, bf16[1024,3200]{1,0:T(8,128)(2,1)}, u32[]{:S(2)}) %copy-start.6) | copy-done | bytes 6553624
  131.8 0.0 copy-start
  131.8 0.0 copy-start.1
  131.8 0.0 copy-start.2
  131.8 0.0 copy-start.3
  131.8 0.0 copy-start.4
  131.8 31.2 %dw_down.1 = bf16[3200,4096]{1,0:T(8,128)(2,1)} custom-call(bf16[1024,3200]{1,0:T(8,128)(2,1)S(1)} %copy-done.6, bf16[1024,4096]{1,0:T(8,128)(2,1)S(1)} %copy-done.5), custom_call_target="tpu_custom_call" | custom-call | flops 26843545600 | bytes 41156608 | tf_op jit(solution)/shard_map/dw_down/pallas_call | solution.py:279
  163.0 0.0 collective-permute-done.2.refs_4_
  163.0 0.0 collective-permute-done.3.refs_5_
  163.0 0.0 copy-done
  163.0 0.0 copy-done.1
  163.0 0.0 copy-done.2
  163.0 0.0 copy-done.3
  163.1 0.0 copy-done.4
  163.1 0.0 copy-start.8
  163.1 30.8 %dw_gate_up.2 = (bf16[4096,3200]{1,0:T(8,128)(2,1)}, bf16[4096,3200]{1,0:T(8,128)(2,1)}) custom-call(bf16[256,4096]{1,0:T(8,128)(2,1)S(1)} %copy-done, bf16[128,4096]{1,0:T(8,128)(2,1)S(1)} %copy-done.1, bf16[128,4096]{1,0:T(8,128)(2,1)S(1)} %copy-done.2, bf16[256,4096]{1,0:T(8,128)(2,1)S(1)} %copy-done.4, ...), custom_call_target="tpu_custom_call" | custom-call | flops 26843545600 | bytes 43515904 | tf_op jit(solution)/shard_map/dw_gate_up/pallas_call | solution.py:305
  193.8 0.0 collective-permute-done
  193.8 0.0 collective-permute-done.1
  193.8 0.0 copy-done.8
  193.8 2.1 add_convert_fusion.2
  195.9 0.1 collective-permute-start.4
  196.1 3.2 %collective-permute-start.5 = (bf16[128,4096]{1,0:T(8,128)(2,1)S(1)}, bf16[128,4096]{1,0:T(8,128)(2,1)S(1)}, u32[]{:S(2)}, u32[]{:S(2)}) collective-permute-start(bf16[128,4096]{1,0:T(8,128)(2,1)S(1)} %get-tuple-element.48), channel_id=1, source_target_pairs={{0,3},{1,0},{2,1},{3,2},{4,7},{5,4},{6,5},{7,6},{8,11},{9,8},{10,9... | collective-permute-start | bytes 3145736 | tf_op jit(solution)/shard_map/ppermute | solution.py:358
  199.3 0.0 copy-start.7
  199.3 30.7 %dw_gate_up.3 = (bf16[4096,3200]{1,0:T(8,128)(2,1)}, bf16[4096,3200]{1,0:T(8,128)(2,1)}) custom-call(bf16[256,4096]{1,0:T(8,128)(2,1)S(1)} %copy-done, bf16[128,4096]{1,0:T(8,128)(2,1)S(1)} %copy-done.1, bf16[128,4096]{1,0:T(8,128)(2,1)S(1)} %copy-done.2, bf16[256,4096]{1,0:T(8,128)(2,1)S(1)} %copy-done.4, ...), custom_call_target="tpu_custom_call", output_to_operand_aliasing={{0}: (7, {}), {1}: (8, {})} | custom-call | flops 26843545600 | bytes 43515904 | tf_op jit(solution)/shard_map/dw_gate_up/pallas_call | solution.py:305
  230.0 0.0 collective-permute-done.4
  230.0 0.0 collective-permute-done.5
  230.0 0.0 copy-done.7
  230.0 2.5 %add_convert_fusion.1 = (bf16[128,4096]{1,0:T(8,128)(2,1)S(1)}, bf16[128,4096]{1,0:T(8,128)(2,1)S(1)}) fusion(bf16[128,4096]{1,0:T(8,128)(2,1)S(1)} %collective-permute-done.4, f32[256,4096]{1,0:T(8,128)S(1)} %copy-done.7, bf16[256,4096]{1,0:T(8,128)(2,1)} %collective-permute-done.1, bf16[128,4096]{1,0:T(8,128)(2,1)S(1)} %collective-permute-done.5, ...), kind=kLoop, calls=%fused_computation.2 | loop fusion | flops 5242880 | bytes 10485760 | tf_op jit(solution)/shard_map/convert_element_type | solution.py:376
  232.5 1.5 pad_maximum_fusion
Async XLA Ops:
  119.0 44.1 %collective-permute-start.2 = (bf16[128,4096]{1,0:T(8,128)(2,1)}, bf16[128,4096]{1,0:T(8,128)(2,1)S(1)}, u32[]{:S(2)}, u32[]{:S(2)}) collective-permute-start(bf16[128,4096]{1,0:T(8,128)(2,1)} %get-tuple-element.33.refs_1_), channel_id=1, source_target_pairs={{0,1},{1,2},{2,3},{3,0},{4,5},{5,6},{6,7},{7,4},{8,9},{9,10},{10,1... | collective-permute-start | bytes 3145736 | tf_op jit(solution)/shard_map/ppermute | solution.py:358
  120.4 42.6 %collective-permute-start.3 = (bf16[128,4096]{1,0:T(8,128)(2,1)}, bf16[128,4096]{1,0:T(8,128)(2,1)S(1)}, u32[]{:S(2)}, u32[]{:S(2)}) collective-permute-start(bf16[128,4096]{1,0:T(8,128)(2,1)} %get-tuple-element.34.refs_2_), channel_id=1, source_target_pairs={{0,3},{1,0},{2,1},{3,2},{4,7},{5,4},{6,5},{7,6},{8,11},{9,8},{10,9... | collective-permute-start | bytes 3145736 | tf_op jit(solution)/shard_map/ppermute | solution.py:358
  122.3 71.5 %collective-permute-start = (bf16[256,4096]{1,0:T(8,128)(2,1)}, bf16[256,4096]{1,0:T(8,128)(2,1)}, u32[]{:S(2)}, u32[]{:S(2)}) collective-permute-start(bf16[256,4096]{1,0:T(8,128)(2,1)} %get-tuple-element.31), channel_id=1, source_target_pairs={{0,1},{1,2},{2,3},{3,0},{4,5},{5,6},{6,7},{7,4},{8,9},{9,10},{10,1... | collective-permute-start | bytes 6291464 | tf_op jit(solution)/shard_map/ppermute | solution.py:358
  122.4 71.4 %collective-permute-start.1 = (bf16[256,4096]{1,0:T(8,128)(2,1)}, bf16[256,4096]{1,0:T(8,128)(2,1)}, u32[]{:S(2)}, u32[]{:S(2)}) collective-permute-start(bf16[256,4096]{1,0:T(8,128)(2,1)} %get-tuple-element.32), channel_id=1, source_target_pairs={{0,3},{1,0},{2,1},{3,2},{4,7},{5,4},{6,5},{7,6},{8,11},{9,8},{10,9... | collective-permute-start | bytes 6291464 | tf_op jit(solution)/shard_map/ppermute | solution.py:358
  125.5 3.4 %copy-start.5 = (bf16[1024,4096]{1,0:T(8,128)(2,1)S(1)}, bf16[1024,4096]{1,0:T(8,128)(2,1)}, u32[]{:S(2)}) copy-start(bf16[1024,4096]{1,0:T(8,128)(2,1)} %get-tuple-element.37.dy_ref) | copy-start | bytes 25165828
  128.9 2.9 %copy-start.6 = (bf16[1024,3200]{1,0:T(8,128)(2,1)S(1)}, bf16[1024,3200]{1,0:T(8,128)(2,1)}, u32[]{:S(2)}) copy-start(bf16[1024,3200]{1,0:T(8,128)(2,1)} %get-tuple-element.36.h_ref) | copy-start | bytes 19660804
  131.8 31.3 %copy-start = (bf16[256,4096]{1,0:T(8,128)(2,1)S(1)}, bf16[256,4096]{1,0:T(8,128)(2,1)}, u32[]{:S(2)}) copy-start(bf16[256,4096]{1,0:T(8,128)(2,1)} %refs_0_.3) | copy-start | bytes 6291460
  131.8 31.3 %copy-start.1 = (bf16[128,4096]{1,0:T(8,128)(2,1)S(1)}, bf16[128,4096]{1,0:T(8,128)(2,1)}, u32[]{:S(2)}) copy-start(bf16[128,4096]{1,0:T(8,128)(2,1)} %get-tuple-element.33.refs_1_) | copy-start | bytes 3145732
  131.8 31.3 %copy-start.2 = (bf16[128,4096]{1,0:T(8,128)(2,1)S(1)}, bf16[128,4096]{1,0:T(8,128)(2,1)}, u32[]{:S(2)}) copy-start(bf16[128,4096]{1,0:T(8,128)(2,1)} %get-tuple-element.34.refs_2_) | copy-start | bytes 3145732
  131.8 31.3 %copy-start.3 = (bf16[1024,6400]{1,0:T(8,128)(2,1)S(1)}, bf16[1024,6400]{1,0:T(8,128)(2,1)}, u32[]{:S(2)}) copy-start(bf16[1024,6400]{1,0:T(8,128)(2,1)} %get-tuple-element.40.refs_6_) | copy-start | bytes 39321604
  131.8 31.3 %copy-start.4 = (bf16[256,4096]{1,0:T(8,128)(2,1)S(1)}, bf16[256,4096]{1,0:T(8,128)(2,1)}, u32[]{:S(2)}) copy-start(bf16[256,4096]{1,0:T(8,128)(2,1)} %get-tuple-element.35.refs_3_) | copy-start | bytes 6291460
  163.1 30.8 %copy-start.8 = (f32[256,4096]{1,0:T(8,128)S(1)}, f32[256,4096]{1,0:T(8,128)}, u32[]{:S(2)}) copy-start(f32[256,4096]{1,0:T(8,128)} %get-tuple-element.30) | copy-start | bytes 12582916
  195.9 34.1 %collective-permute-start.4 = (bf16[128,4096]{1,0:T(8,128)(2,1)S(1)}, bf16[128,4096]{1,0:T(8,128)(2,1)S(1)}, u32[]{:S(2)}, u32[]{:S(2)}) collective-permute-start(bf16[128,4096]{1,0:T(8,128)(2,1)S(1)} %get-tuple-element.47), channel_id=1, source_target_pairs={{0,1},{1,2},{2,3},{3,0},{4,5},{5,6},{6,7},{7,4},{8,9},{9,10},{10,1... | collective-permute-start | bytes 3145736 | tf_op jit(solution)/shard_map/ppermute | solution.py:358
  196.1 34.0 %collective-permute-start.5 = (bf16[128,4096]{1,0:T(8,128)(2,1)S(1)}, bf16[128,4096]{1,0:T(8,128)(2,1)S(1)}, u32[]{:S(2)}, u32[]{:S(2)}) collective-permute-start(bf16[128,4096]{1,0:T(8,128)(2,1)S(1)} %get-tuple-element.48), channel_id=1, source_target_pairs={{0,3},{1,0},{2,1},{3,2},{4,7},{5,4},{6,5},{7,6},{8,11},{9,8},{10,9... | collective-permute-start | bytes 3145736 | tf_op jit(solution)/shard_map/ppermute | solution.py:358
  199.3 30.7 %copy-start.7 = (f32[256,4096]{1,0:T(8,128)S(1)}, f32[256,4096]{1,0:T(8,128)}, u32[]{:S(2)}) copy-start(f32[256,4096]{1,0:T(8,128)} %get-tuple-element.29) | copy-start | bytes 12582916
